TPU v7x, 32 devices: a whole 2x2x4 slice. The times are simulated.
32 devices in a mesh: depth: 2 (over x), lat: 16 (over z, y, core).
Axes of the slice: x: 2, y: 2, z: 4, core: 2. Of those that a mesh axis runs over, the one named last changes fastest.
Arguments:
- displacement: float32 [3, 16, 128, 256], P(None, 'depth', 'lat'), may hold values from -6 to 6
- velocity: float32 [3, 16, 128, 256], P(None, 'depth', 'lat'), may hold values from -6 to 6
- inverse_mass: float32 [16, 128, 256], P('depth', 'lat'), may hold values from 0.5 to 2
- material: int32 [16, 128, 256], P('depth', 'lat'), may hold values from 0 to 7
- dilation_table: float32 [8], replicated, may hold values from 0.5 to 2
- shear_table: float32 [8], replicated, may hold values from 0.5 to 2
- stiffness_pair: float32 [2, 24, 24], replicated, may hold values from -1.5 to 3.5, as said below
- impedance: float32 [3], replicated, may hold values from 0.5 to 2
- bedrock_mask: int32 [128, 256], P('lat'), may hold values 0 or 1
- incident: float32 [6, 3, 128, 256], P(None, None, 'lat'), may hold values from -6 to 6
Outputs:
- new_displacement: float32 [3, 16, 128, 256], P(None, 'depth', 'lat')
- new_velocity: float32 [3, 16, 128, 256], P(None, 'depth', 'lat')
Inputs may be any that keep to these rules, and one draw needn't show every extreme that they name: `stiffness_pair`: symmetric positive definite.
All inputs are finite; a program needn't handle non-finite values. No bound on the sum of `bedrock_mask` on one device may be relied on, other than what follows from the above.
Results may differ from a plain program's by a relative error of at most 0.00016.
Values sent between devices are 32-bit elements; how exact they have to be, the bound alone decides.
A program may use at most 64 MiB of HBM per device.

v0:
```python
import functools

import jax
import jax.numpy as jnp
from jax import lax
from jax.experimental import pallas as pl
from jax.experimental.pallas import tpu as pltpu
from jax.sharding import PartitionSpec as P

time_step = 0.1
WIDTH = 2
f32 = jnp.float32
bf16 = jnp.bfloat16


def kernel(
    cfg, dil_tab, shr_tab, imp_ref, disp, vel, inv, mat, stiff, mask, inc, out_d, out_v,
    tiles, split, moduli, carry, pull, land_y, land_z, land_c, big_s,
    send_sem, recv_sem, q_send, q_recv,
):
    nz, ny, nx, steps, depths, lats, w = cfg
    h = w
    nh = nx // 128
    ext_z = nz + 2 * h
    ext_y = tiles.shape[2] // 8
    nmat = dil_tab.shape[0]
    di = lax.axis_index("depth")
    li = lax.axis_index("lat")
    exists = {}
    for dz in (-1, 0, 1):
        for dy in (-1, 0, 1):
            if dz == 0 and dy == 0:
                continue
            if (dz != 0 and depths == 1) or (dy != 0 and lats == 1):
                continue
            exists[(dz, dy)] = (
                (di + dz >= 0) & (di + dz < depths) & (li + dy >= 0) & (li + dy < lats)
            )
    dirs = list(exists)
    is_bottom = di == depths - 1
    extra = [w - 1 - s % w for s in range(steps)]
    if steps % w:
        for s in range(steps - steps % w, steps):
            extra[s] = steps - 1 - s
    wide = [s for s in range(steps) if extra[s] > 0]
    order = wide + [s for s in range(steps) if extra[s] == 0]
    q_of = {s: i for i, s in enumerate(order)}

    pull[...] = jnp.zeros_like(pull)
    barrier = pltpu.get_barrier_semaphore()
    for dz, dy in dirs:
        @pl.when(exists[(dz, dy)])
        def _(dz=dz, dy=dy):
            pl.semaphore_signal(
                barrier, inc=1, device_id={"depth": di + dz, "lat": li + dy},
                device_id_type=pl.DeviceIdType.MESH,
            )

    def zero_layer(z, c):
        tiles[z] = jnp.zeros(tiles.shape[1:], f32)
        split[z] = jnp.zeros(split.shape[1:], bf16)
        return c

    lax.fori_loop(0, ext_z, zero_layer, 0)

    def fill_layer(z, c):
        for hf in range(nh):
            lanes = slice(hf * 128, hf * 128 + 128)
            for comp in range(3):
                tiles[h + z, hf, pl.ds(h * 8 + comp, ny, stride=8), :] = disp[comp, z, :, lanes]
                tiles[h + z, hf, pl.ds(h * 8 + 3 + comp, ny, stride=8), :] = vel[comp, z, :, lanes]
            tiles[h + z, hf, pl.ds(h * 8 + 6, ny, stride=8), :] = inv[z, :, lanes] * (-time_step)
            tiles[h + z, hf, pl.ds(h * 8 + 7, ny, stride=8), :] = (mat[z, :, lanes] + 1).astype(f32)
        return c

    lax.fori_loop(0, nz, fill_layer, 0)

    @pl.when(is_bottom)
    def _():
        for hf in range(nh):
            lanes = slice(hf * 128, hf * 128 + 128)
            twice = 2.0 * mask[:, lanes].astype(f32)
            for s in range(steps):
                for comp in range(3):
                    pull[q_of[s], hf, pl.ds(h * 8 + 3 + comp, ny, stride=8), :] = (
                        imp_ref[comp] * (twice * inc[s, comp, :, lanes])
                    )

    pl.semaphore_wait(barrier, sum(jnp.where(here, 1, 0) for here in exists.values()))

    def piece(n, dz, dy):
        zs = pl.ds({-1: h, 0: h, 1: h + nz - w}[dz], nz if dz == 0 else w)
        ys = pl.ds({-1: h, 0: h, 1: h + ny - w}[dy] * 8, (ny if dy == 0 else w) * 8)
        if dz == 0:
            dst = land_y.at[n, (1 - dy) // 2]
        elif dy == 0:
            dst = land_z.at[n, (1 - dz) // 2]
        else:
            dst = land_c.at[n, (1 - dz) // 2 * 2 + (1 - dy) // 2]
        k = dirs.index((dz, dy))
        back = dirs.index((-dz, -dy))
        return pltpu.make_async_remote_copy(
            src_ref=tiles.at[zs, :, ys, :],
            dst_ref=dst,
            send_sem=send_sem.at[n, k],
            recv_sem=recv_sem.at[n, back],
            device_id={"depth": di + dz, "lat": li + dy},
            device_id_type=pl.DeviceIdType.MESH,
        )

    def arrived(n, dz, dy):
        if dz == 0:
            dst = land_y.at[n, (1 + dy) // 2]
        elif dy == 0:
            dst = land_z.at[n, (1 + dz) // 2]
        else:
            dst = land_c.at[n, (1 + dz) // 2 * 2 + (1 + dy) // 2]
        k = dirs.index((dz, dy))
        return dst, pltpu.make_async_remote_copy(
            src_ref=dst, dst_ref=dst, send_sem=send_sem.at[n, k], recv_sem=recv_sem.at[n, k],
            device_id={"depth": di + dz, "lat": li + dy},
            device_id_type=pl.DeviceIdType.MESH,
        )

    def pull_copy(dy, waits=False):
        src = pl.ds((h if dy < 0 else h + ny - (w - 1)) * 8, (w - 1) * 8)
        dst = pl.ds((h + ny if dy < 0 else h - (w - 1)) * 8, (w - 1) * 8)
        side = (1 + dy) // 2
        return pltpu.make_async_remote_copy(
            src_ref=pull.at[pl.ds(0, len(wide)), :, src, :],
            dst_ref=pull.at[pl.ds(0, len(wide)), :, dst, :],
            send_sem=q_send.at[side],
            recv_sem=q_recv.at[side if waits else 1 - side],
            device_id={"depth": di, "lat": li + dy},
            device_id_type=pl.DeviceIdType.MESH,
        )

    pull_dirs = [dy for dy in (-1, 1) if w > 1 and (0, dy) in exists]

    def start_all(n):
        for dz, dy in sorted(dirs, key=lambda d: -abs(d[0]) - abs(d[1])):
            @pl.when(exists[(dz, dy)])
            def _(dz=dz, dy=dy):
                piece(n, dz, dy).start()

    rows = lax.broadcasted_iota(jnp.int32, (8, nx), 0)
    columns = lax.broadcasted_iota(jnp.int32, (8, nx), 1)
    top3 = rows < 3
    mid3 = (rows >= 3) & (rows < 6)
    last = columns == nx - 1
    first_column = columns == 0
    keep_in = jnp.where(last, 0.0, 1.0)
    keep_out = jnp.where(first_column, 0.0, 1.0)

    def load_tile(z, y):
        return jnp.concatenate([tiles[z, hf, pl.ds(y * 8, 8), :] for hf in range(nh)], 1)

    def put_split(z, y, tile):
        beside = pltpu.roll(pltpu.roll(tile, nx - 1, 1), 3, 0) * keep_in
        both = jnp.where(top3, tile, beside)
        high = both.astype(bf16).astype(f32)
        split[z, y] = jnp.concatenate([high, both - high], 0).astype(bf16)

    def receive(n, dz, dy):
        @pl.when(exists[(dz, dy)])
        def _():
            ref, copy = arrived(n, dz, dy)
            copy.wait_recv()
            z0 = {-1: 0, 0: h, 1: h + nz}[dz]
            y0 = {-1: 0, 0: h, 1: h + ny}[dy]
            yn = ny if dy == 0 else w

            def body(z, c):
                for y in range(yn):
                    parts = [ref[z, hf, pl.ds(y * 8, 8), :] for hf in range(nh)]
                    for hf in range(nh):
                        tiles[z0 + z, hf, pl.ds((y0 + y) * 8, 8), :] = parts[hf]
                    put_split(z0 + z, y0 + y, jnp.concatenate(parts, 1))
                return c

            lax.fori_loop(0, nz if dz == 0 else w, body, 0)

    def sent(n):
        for dz, dy in dirs:
            @pl.when(exists[(dz, dy)])
            def _(dz=dz, dy=dy):
                piece(n, dz, dy).wait_send()

    def layer(z, e, s, opening):
        ya, yb = h - 1 - e, h + ny - 1 + e
        if not opening:
            @pl.when(is_bottom & (z == h + nz - 1))
            def _():
                wet = jnp.where(rows == 3, imp_ref[0], jnp.where(rows == 4, imp_ref[1], imp_ref[2]))
                for y in range(ya + 1, yb + 1):
                    pulled = jnp.concatenate(
                        [pull[q_of[s], hf, pl.ds(y * 8, 8), :] for hf in range(nh)], 1
                    )
                    carry[y] += jnp.where(mid3, wet * load_tile(z, y) - pulled, 0.0)

        matrix = big_s[...]
        prev_low = prev_high = None
        for y in range(ya, yb + 1):
            values = jnp.concatenate(
                [split[z, y], split[z, y + 1], split[z + 1, y], split[z + 1, y + 1]], 0
            )
            values = jnp.concatenate([values, values], 0)
            product = jnp.dot(matrix, values, preferred_element_type=f32)
            dil = jnp.concatenate([moduli[0, z, hf, pl.ds(y, 1), :] for hf in range(nh)], 1)
            shr = jnp.concatenate([moduli[1, z, hf, pl.ds(y, 1), :] for hf in range(nh)], 1)
            g = dil * product[0:32] + shr * product[32:64]
            if y > ya:
                high = g[16:24] + prev_high
                if not opening:
                    force = (g[0:8] + prev_low) + carry[y]
                    side = pltpu.roll(pltpu.roll(force, 1, 1), 3, 0) * keep_out
                    tile = load_tile(z, y)
                    mass = jnp.concatenate(
                        [tiles[z, hf, pl.ds(y * 8 + 6, 1), :] for hf in range(nh)], 1
                    )
                    moved = tile + jnp.where(mid3, mass * (force + side), 0.0)
                    tile = moved + jnp.where(top3, time_step * pltpu.roll(moved, 5, 0), 0.0)
                    for hf in range(nh):
                        tiles[z, hf, pl.ds(y * 8, 8), :] = tile[:, hf * 128 : hf * 128 + 128]
                    if s < steps - 1:
                        put_split(z, y, tile)
                carry[y] = high
            prev_low, prev_high = g[8:16], g[24:32]

    start_all(0)
    for dy in pull_dirs:
        @pl.when(exists[(0, dy)] & is_bottom)
        def _(dy=dy):
            pull_copy(dy).start()

    i32 = jnp.int32
    ri = lax.broadcasted_iota(i32, (32, 24), 0)
    rc = lax.broadcasted_iota(i32, (32, 24), 1)
    r8 = ri % 8
    left = (r8 < 6) & (rc == (ri // 8) * 6 + jnp.where(r8 < 3, r8 + 3, r8 - 3))
    left = jnp.where(left, 1.0, 0.0).astype(bf16)
    ci = lax.broadcasted_iota(i32, (24, 64), 0)
    cc = lax.broadcasted_iota(i32, (24, 64), 1)
    right = (cc % 8 < 6) & (ci == (cc // 16) * 6 + cc % 8)
    right = jnp.where(right, 1.0, 0.0).astype(bf16)
    blocks = []
    for m in range(2):
        whole = stiff[m]
        upper = whole.astype(bf16)
        lower = (whole - upper.astype(f32)).astype(bf16)
        parts = []
        for part in (upper, lower):
            picked = jnp.dot(left, part, preferred_element_type=f32).astype(bf16)
            parts.append(jnp.dot(picked, right, preferred_element_type=f32))
        blocks.append(jnp.concatenate(parts, 1))
    big_s[...] = jnp.concatenate(blocks, 0).astype(bf16)

    def split_layer(z, c):
        for y in range(ny):
            put_split(h + z, h + y, load_tile(h + z, h + y))
        return c

    lax.fori_loop(0, nz, split_layer, 0)

    def lookup(z, c):
        for hf in range(nh):
            for y0 in range(0, ext_y, 8):
                kind = tiles[z, hf, pl.ds(y0 * 8 + 7, 8, stride=8), :]
                dil = jnp.zeros((8, 128), f32)
                shr = jnp.zeros((8, 128), f32)
                for m in range(nmat):
                    hit = kind == float(m + 1)
                    dil = jnp.where(hit, dil_tab[m], dil)
                    shr = jnp.where(hit, shr_tab[m], shr)
                moduli[0, z, hf, pl.ds(y0, 8), :] = dil
                moduli[1, z, hf, pl.ds(y0, 8), :] = shr
        return c

    for s in range(steps):
        n, e = s // w, extra[s]
        if s % w == 0:
            if s > 0:
                start_all(n)
            for dz, dy in dirs:
                receive(n, dz, dy)
            sent(n)
            if s == 0:
                for dy in pull_dirs:
                    @pl.when(exists[(0, dy)] & is_bottom)
                    def _(dy=dy):
                        pull_copy(dy).wait_send()
                        pull_copy(dy, True).wait_recv()
                lax.fori_loop(0, ext_z, lookup, 0)
        if depths == 1:
            start, count = h, nz
        elif depths == 2:
            start, count = jnp.where(di == 0, h, h - e), nz + e
        else:
            start, count = h - e, nz + 2 * e
        layer(start - 1, e, s, True)

        def body(z, c, start=start, e=e, s=s):
            layer(start + z, e, s, False)
            return c

        lax.fori_loop(0, count, body, 0)

    def give(z, c):
        for hf in range(nh):
            lanes = slice(hf * 128, hf * 128 + 128)
            for comp in range(3):
                out_d[comp, z, :, lanes] = tiles[h + z, hf, pl.ds(h * 8 + comp, ny, stride=8), :]
                out_v[comp, z, :, lanes] = tiles[h + z, hf, pl.ds(h * 8 + 3 + comp, ny, stride=8), :]
        return c

    lax.fori_loop(0, nz, give, 0)


def solution(mesh):
    depths, lats = mesh.shape["depth"], mesh.shape["lat"]

    def per_device(disp, vel, inv, mat, dil_tab, shr_tab, stiff, imp, mask, inc):
        _, nz, ny, nx = disp.shape
        steps = inc.shape[0]
        w = min(WIDTH, nz, ny, steps)
        nh = nx // 128
        groups = -(-steps // w)
        ext_z = nz + 2 * w
        ext_y = -(-(ny + 2 * w) // 8) * 8
        ndirs = (3 if depths > 1 else 1) * (3 if lats > 1 else 1) - 1
        smem = pl.BlockSpec(memory_space=pltpu.SMEM)
        vmem = pl.BlockSpec(memory_space=pltpu.VMEM)
        shape = jax.ShapeDtypeStruct(disp.shape, f32)
        return pl.pallas_call(
            functools.partial(kernel, (nz, ny, nx, steps, depths, lats, w)),
            out_shape=(shape, shape),
            in_specs=[smem] * 3 + [vmem] * 7,
            out_specs=(vmem, vmem),
            scratch_shapes=[
                pltpu.VMEM((ext_z, nh, ext_y * 8, 128), f32),
                pltpu.VMEM((ext_z, ext_y, 16, nx), bf16),
                pltpu.VMEM((2, ext_z, nh, ext_y, 128), f32),
                pltpu.VMEM((ext_y, 8, nx), f32),
                pltpu.VMEM((steps, nh, ext_y * 8, 128), f32),
                pltpu.VMEM((groups, 2, nz, nh, w * 8, 128), f32),
                pltpu.VMEM((groups, 2, w, nh, ny * 8, 128), f32),
                pltpu.VMEM((groups, 4, w, nh, w * 8, 128), f32),
                pltpu.VMEM((64, 128), bf16),
                pltpu.SemaphoreType.DMA((groups, ndirs)),
                pltpu.SemaphoreType.DMA((groups, ndirs)),
                pltpu.SemaphoreType.DMA((2,)),
                pltpu.SemaphoreType.DMA((2,)),
            ],
            compiler_params=pltpu.CompilerParams(
                collective_id=0, has_side_effects=True, vmem_limit_bytes=56 * 1024 * 1024
            ),
        )(dil_tab, shr_tab, imp, disp, vel, inv, mat, stiff, mask, inc)

    field = P(None, "depth", "lat", None)
    node = P("depth", "lat", None)
    in_specs = (field, field, node, node, P(), P(), P(), P(), P("lat", None), P(None, None, "lat", None))
    return jax.shard_map(
        per_device, mesh=mesh, in_specs=in_specs, out_specs=(field, field), check_vma=False
    )
```

profile of v0, /device:TPU:19, one launch (start us, length us, event | category | flops | bytes accessed | tf_op | source)
XLA Modules:
  0.0 50.6 jit_solution(6780563536742482447)
XLA Ops:
  0.6 47.6 %shard_map.113 = (f32[3,8,8,256]{3,2,1,0:T(8,128)}, f32[3,8,8,256]{3,2,1,0:T(8,128)}) custom-call(f32[8]{0:T(128)} %dil_tab.1, f32[8]{0:T(128)} %shr_tab.1, f32[3]{0:T(128)} %imp_ref.1, f32[3,8,8,256]{3,2,1,0:T(8,128)} %disp.1, f32[3,8,8,256]{3,2,1,0:T(8,128)} %vel.1, f32[8,8,256]{2,1,0:T(8,128)} %inv.1, s32[8,8,256]{2,1,0:T(8,128)} %mat.1, ...), custom_call_target="tpu_custom_call" | custom-call | tf_op jit(solution)/shard_map/pallas_call | solution.py:334
  48.2 0.0 copy-start
  48.3 1.7 %copy.14 = f32[3,8,8,256]{3,2,1,0:T(8,128)} copy(f32[3,8,8,256]{3,2,1,0:T(8,128)} %get-tuple-element.4) | data formatting | bytes 393216
  49.9 0.0 copy-done
  49.9 0.7 %copy.15 = f32[3,8,8,256]{3,2,1,0:T(8,128)} copy(f32[3,8,8,256]{3,2,1,0:T(8,128)S(1)} %copy-done) | data formatting | bytes 393216
Async XLA Ops:
  48.2 1.7 %copy-start = (f32[3,8,8,256]{3,2,1,0:T(8,128)S(1)}, f32[3,8,8,256]{3,2,1,0:T(8,128)}, u32[]{:S(2)}) copy-start(f32[3,8,8,256]{3,2,1,0:T(8,128)} %get-tuple-element.5) | copy-start | bytes 589828
where the time goes:
time: 50.8 us; the launch traced here: 50.6 us
  Pallas kernels  47.6 us (94%)
  local copies, waits for them, and re-layouts  2.34 us (5%)
  between operations  0.65 us (1%)
    pallas_call x1, Pallas kernels, per_device(): pl.pallas_call(functools.partial(kernel, (nz, ny, nx, steps, depths, lats...  47.6 us
    unnamed x4, local copies, waits for them, and re-layouts  2.34 us

commit v1 on v0

v1 whole, which is shorter than its diff:
```python
import functools

import jax
import jax.numpy as jnp
from jax import lax
from jax.experimental import pallas as pl
from jax.experimental.pallas import tpu as pltpu
from jax.sharding import PartitionSpec as P

time_step = 0.1
WIDTH = 2
f32 = jnp.float32
bf16 = jnp.bfloat16


def kernel(
    cfg, dil_tab, shr_tab, imp_ref, disp, vel, inv, mat, stiff, mask, inc, out_d, out_v,
    grid5, split, moduli, carry, held, pull, land_y, land_z, land_c, big_s,
    send_sem, recv_sem, q_send, q_recv,
):
    nz, ny, nx, steps, depths, lats, w = cfg
    h = w
    nh = nx // 128
    hy = -(-h // 8) * 8
    ext_z = nz + 2 * h
    ext_y = grid5.shape[2]
    tiles = grid5.reshape(ext_z, nh, ext_y * 8, 128)
    nmat = dil_tab.shape[0]
    di = lax.axis_index("depth")
    li = lax.axis_index("lat")
    exists = {}
    for dz in (-1, 0, 1):
        for dy in (-1, 0, 1):
            if dz == 0 and dy == 0:
                continue
            if (dz != 0 and depths == 1) or (dy != 0 and lats == 1):
                continue
            exists[(dz, dy)] = (
                (di + dz >= 0) & (di + dz < depths) & (li + dy >= 0) & (li + dy < lats)
            )
    dirs = list(exists)
    is_bottom = di == depths - 1
    extra = [w - 1 - s % w for s in range(steps)]
    if steps % w:
        for s in range(steps - steps % w, steps):
            extra[s] = steps - 1 - s
    wide = [s for s in range(steps) if extra[s] > 0]
    order = wide + [s for s in range(steps) if extra[s] == 0]
    q_of = {s: i for i, s in enumerate(order)}

    pull[...] = jnp.zeros_like(pull)
    barrier = pltpu.get_barrier_semaphore()
    for dz, dy in dirs:
        @pl.when(exists[(dz, dy)])
        def _(dz=dz, dy=dy):
            pl.semaphore_signal(
                barrier, inc=1, device_id={"depth": di + dz, "lat": li + dy},
                device_id_type=pl.DeviceIdType.MESH,
            )

    def fill_layer(z, c):
        for hf in range(nh):
            lanes = slice(hf * 128, hf * 128 + 128)
            for comp in range(3):
                tiles[h + z, hf, pl.ds(hy * 8 + comp, ny, stride=8), :] = disp[comp, z, :, lanes]
                tiles[h + z, hf, pl.ds(hy * 8 + 4 + comp, ny, stride=8), :] = vel[comp, z, :, lanes]
            tiles[h + z, hf, pl.ds(hy * 8 + 3, ny, stride=8), :] = (mat[z, :, lanes] + 1).astype(f32)
            tiles[h + z, hf, pl.ds(hy * 8 + 7, ny, stride=8), :] = inv[z, :, lanes] * (-time_step)
        return c

    lax.fori_loop(0, nz, fill_layer, 0)

    @pl.when(is_bottom)
    def _():
        for hf in range(nh):
            lanes = slice(hf * 128, hf * 128 + 128)
            twice = 2.0 * mask[:, lanes].astype(f32)
            for s in range(steps):
                for comp in range(3):
                    pull[q_of[s], hf, pl.ds(hy * 8 + 4 + comp, ny, stride=8), :] = (
                        imp_ref[comp] * (twice * inc[s, comp, :, lanes])
                    )

    pl.semaphore_wait(barrier, sum(jnp.where(here, 1, 0) for here in exists.values()))

    def landing(n, dz, dy):
        if dz == 0:
            return land_y.at[n, (1 + dy) // 2]
        if dy == 0:
            return land_z.at[n, (1 + dz) // 2]
        return land_c.at[n, (1 + dz) // 2 * 2 + (1 + dy) // 2]

    def span(shift, length, base, width, outward):
        if shift == 0:
            return pl.ds(base, length)
        if outward:
            return pl.ds(0, width) if shift > 0 else pl.ds(w - width, width)
        return pl.ds(base, width) if shift < 0 else pl.ds(base + length - width, width)

    def parts_of(n):
        fields = [(0, w, pl.ds(0, 4 if n == 0 else 3))]
        if w > 1 or n == 0:
            fields.append((1, w - 1 if w > 1 else w, pl.ds(4, 4 if n == 0 else 3)))
        return fields

    def pieces(n, dz, dy, waits=False):
        k, back = dirs.index((dz, dy)), dirs.index((-dz, -dy))
        copies = []
        for f, width, sub in parts_of(n):
            here = landing(n, dz, dy).at[
                span(dz, nz, 0, width, True), :, span(dy, ny, 0, width, True), sub, :
            ]
            there = landing(n, -dz, -dy).at[
                span(-dz, nz, 0, width, True), :, span(-dy, ny, 0, width, True), sub, :
            ]
            mine = grid5.at[
                span(dz, nz, h, width, False), :, span(dy, ny, hy, width, False), sub, :
            ]
            copies.append(
                pltpu.make_async_remote_copy(
                    src_ref=here if waits else mine,
                    dst_ref=here if waits else there,
                    send_sem=send_sem.at[n, k, f],
                    recv_sem=recv_sem.at[n, k if waits else back, f],
                    device_id={"depth": di + dz, "lat": li + dy},
                    device_id_type=pl.DeviceIdType.MESH,
                )
            )
        return copies

    def pull_copy(dy, waits=False):
        src = pl.ds((hy if dy < 0 else hy + ny - (w - 1)) * 8, (w - 1) * 8)
        dst = pl.ds((hy + ny if dy < 0 else hy - (w - 1)) * 8, (w - 1) * 8)
        side = (1 + dy) // 2
        return pltpu.make_async_remote_copy(
            src_ref=pull.at[pl.ds(0, len(wide)), :, src, :],
            dst_ref=pull.at[pl.ds(0, len(wide)), :, dst, :],
            send_sem=q_send.at[side],
            recv_sem=q_recv.at[side if waits else 1 - side],
            device_id={"depth": di, "lat": li + dy},
            device_id_type=pl.DeviceIdType.MESH,
        )

    pull_dirs = [dy for dy in (-1, 1) if w > 1 and (0, dy) in exists]

    def start_all(n):
        for dz, dy in sorted(dirs, key=lambda d: -abs(d[0]) - abs(d[1])):
            @pl.when(exists[(dz, dy)])
            def _(dz=dz, dy=dy):
                for copy in pieces(n, dz, dy):
                    copy.start()

    rows = lax.broadcasted_iota(jnp.int32, (8, nx), 0)
    columns = lax.broadcasted_iota(jnp.int32, (8, nx), 1)
    top3 = rows < 3
    mid3 = (rows >= 4) & (rows < 7)
    inner = (rows < 6) & (columns < nx - 1)
    keep_out = columns > 0

    def load_tile(z, y):
        return jnp.concatenate([tiles[z, hf, pl.ds(y * 8, 8), :] for hf in range(nh)], 1)

    def put_split(z, y, tile):
        beside = pltpu.roll(pltpu.roll(tile, 3, 0), nx - 1, 1)
        both = jnp.where(top3, tile, jnp.where(inner, beside, 0.0))
        high = both.astype(bf16).astype(f32)
        split[z, y] = jnp.concatenate([high, both - high], 0).astype(bf16)

    def receive(n, dz, dy):
        z0 = {-1: 0, 0: h, 1: h + nz}[dz]
        y0 = {-1: hy - w, 0: hy, 1: hy + ny}[dy]
        zn, yn = nz if dz == 0 else w, ny if dy == 0 else w
        ref = landing(n, dz, dy)

        if n == 0:
            @pl.when(jnp.logical_not(exists[(dz, dy)]))
            def _():
                def clear(z, c):
                    for y in range(yn):
                        for hf in range(nh):
                            tiles[z0 + z, hf, pl.ds((y0 + y) * 8, 8), :] = jnp.zeros((8, 128), f32)
                        split[z0 + z, y0 + y] = jnp.zeros((16, nx), bf16)
                    return c

                lax.fori_loop(0, zn, clear, 0)

        @pl.when(exists[(dz, dy)])
        def _():
            for copy in pieces(n, dz, dy, True):
                copy.wait_recv()
            far_y = {-1: 0, 0: -1, 1: w - 1}[dy]

            def body(z, c):
                far_z = (z == 0) if dz < 0 else (z == w - 1)
                for y in range(yn):
                    new = jnp.concatenate([ref[z, hf, y, :, :] for hf in range(nh)], 1)
                    low = rows < (4 if n == 0 else 3)
                    full = (low | (rows >= 4)) if n == 0 else (low | mid3)
                    if w == 1:
                        valid = full if n == 0 else low
                    elif y == far_y:
                        valid = low
                    elif dz == 0:
                        valid = full
                    else:
                        valid = low | (full & jnp.logical_not(far_z))
                    old = jnp.zeros((8, nx), f32) if n == 0 else load_tile(z0 + z, y0 + y)
                    new = jnp.where(valid, new, old)
                    for hf in range(nh):
                        tiles[z0 + z, hf, pl.ds((y0 + y) * 8, 8), :] = new[:, hf * 128 : hf * 128 + 128]
                    put_split(z0 + z, y0 + y, new)
                return c

            lax.fori_loop(0, zn, body, 0)

    def sent(n):
        for dz, dy in dirs:
            @pl.when(exists[(dz, dy)])
            def _(dz=dz, dy=dy):
                for copy in pieces(n, dz, dy):
                    copy.wait_send()

    wet = jnp.where(rows == 4, imp_ref[0], jnp.where(rows == 5, imp_ref[1], imp_ref[2]))
    wet = jnp.where(mid3 & is_bottom, wet, 0.0)

    def products(z, e, opening):
        ya, yb = hy - 1 - e, hy + ny - 1 + e
        matrix = big_s[...]
        prev_low = prev_high = None
        results = []
        for y in range(ya, yb + 1):
            values = jnp.concatenate(
                [split[z, y], split[z, y + 1], split[z + 1, y], split[z + 1, y + 1]], 0
            )
            values = jnp.concatenate([values, values], 0)
            product = jnp.dot(matrix, values, preferred_element_type=f32)
            dil = jnp.concatenate([moduli[0, z, hf, pl.ds(y, 1), :] for hf in range(nh)], 1)
            shr = jnp.concatenate([moduli[1, z, hf, pl.ds(y, 1), :] for hf in range(nh)], 1)
            g = dil * product[0:32] + shr * product[32:64]
            if y > ya:
                low = None if opening else (g[0:8] + prev_low) + carry[y]
                results.append((y, low, g[16:24] + prev_high))
            prev_low, prev_high = g[8:16], g[24:32]
        return results

    def keep(results):
        for y, low, high in results:
            if low is not None:
                held[y] = low
            carry[y] = high

    def update(z, e, s, closing):
        for y in range(hy - e, hy + ny + e):
            force = held[y]
            tile = load_tile(z, y)
            if closing:
                pulled = jnp.concatenate(
                    [pull[q_of[s], hf, pl.ds(y * 8, 8), :] for hf in range(nh)], 1
                )
                force = force + (wet * tile - pulled)
            side = pltpu.roll(pltpu.roll(force, 4, 0), 1, 1)
            mass = jnp.concatenate(
                [tiles[z, hf, pl.ds(y * 8 + 7, 1), :] for hf in range(nh)], 1
            )
            whole = force + jnp.where(keep_out, side, 0.0)
            moved = tile + jnp.where(mid3, mass * whole, 0.0)
            tile = moved + jnp.where(top3, time_step * pltpu.roll(moved, 4, 0), 0.0)
            for hf in range(nh):
                tiles[z, hf, pl.ds(y * 8, 8), :] = tile[:, hf * 128 : hf * 128 + 128]
            if s < steps - 1:
                put_split(z, y, tile)

    start_all(0)
    for dy in pull_dirs:
        @pl.when(exists[(0, dy)] & is_bottom)
        def _(dy=dy):
            pull_copy(dy).start()

    i32 = jnp.int32
    ri = lax.broadcasted_iota(i32, (32, 24), 0)
    rc = lax.broadcasted_iota(i32, (32, 24), 1)
    r8 = ri % 8
    left = (r8 % 4 < 3) & (rc == (ri // 8) * 6 + jnp.where(r8 < 3, r8 + 3, r8 - 4))
    left = jnp.where(left, 1.0, 0.0).astype(bf16)
    ci = lax.broadcasted_iota(i32, (24, 64), 0)
    cc = lax.broadcasted_iota(i32, (24, 64), 1)
    right = (cc % 8 < 6) & (ci == (cc // 16) * 6 + cc % 8)
    right = jnp.where(right, 1.0, 0.0).astype(bf16)
    blocks = []
    for m in range(2):
        whole = stiff[m]
        upper = whole.astype(bf16)
        lower = (whole - upper.astype(f32)).astype(bf16)
        parts = []
        for part in (upper, lower):
            picked = jnp.dot(left, part, preferred_element_type=f32).astype(bf16)
            parts.append(jnp.dot(picked, right, preferred_element_type=f32))
        blocks.append(jnp.concatenate(parts, 1))
    big_s[...] = jnp.concatenate(blocks, 0).astype(bf16)

    def split_layer(z, c):
        for y in range(ny):
            put_split(h + z, hy + y, load_tile(h + z, hy + y))
        return c

    lax.fori_loop(0, nz, split_layer, 0)

    own_chunks = [y0 for y0 in range(0, ext_y, 8) if hy <= y0 and y0 + 8 <= hy + ny]
    other_chunks = [y0 for y0 in range(0, ext_y, 8) if y0 not in own_chunks]

    def lookup(chunks):
        def body(z, c):
            for hf in range(nh):
                for y0 in chunks:
                    kind = tiles[z, hf, pl.ds(y0 * 8 + 3, 8, stride=8), :]
                    dil = jnp.zeros((8, 128), f32)
                    shr = jnp.zeros((8, 128), f32)
                    for m in range(nmat):
                        hit = kind == float(m + 1)
                        dil = jnp.where(hit, dil_tab[m], dil)
                        shr = jnp.where(hit, shr_tab[m], shr)
                    moduli[0, z, hf, pl.ds(y0, 8), :] = dil
                    moduli[1, z, hf, pl.ds(y0, 8), :] = shr
            return c

        return body

    lax.fori_loop(h, h + nz, lookup(own_chunks), 0)

    for s in range(steps):
        n, e = s // w, extra[s]
        if s % w == 0:
            if s > 0:
                start_all(n)
            for dz, dy in dirs:
                receive(n, dz, dy)
            sent(n)
            if s == 0:
                for dy in pull_dirs:
                    @pl.when(exists[(0, dy)] & is_bottom)
                    def _(dy=dy):
                        pull_copy(dy).wait_send()
                        pull_copy(dy, True).wait_recv()
                lax.fori_loop(0, h, lookup(own_chunks + other_chunks), 0)
                lax.fori_loop(h + nz, ext_z, lookup(own_chunks + other_chunks), 0)
                lax.fori_loop(h, h + nz, lookup(other_chunks), 0)
        start = jnp.where(di == 0, h, h - e)
        stop = jnp.where(is_bottom, h + nz - 1, h + nz - 1 + e)
        keep(products(start - 1, e, True))
        keep(products(start, e, False))

        def body(z, c, e=e, s=s):
            results = products(z, e, False)
            update(z - 1, e, s, False)
            keep(results)
            return c

        lax.fori_loop(start + 1, stop + 1, body, 0)
        update(stop, e, s, True)

    def give(z, c):
        for hf in range(nh):
            lanes = slice(hf * 128, hf * 128 + 128)
            for comp in range(3):
                out_d[comp, z, :, lanes] = tiles[h + z, hf, pl.ds(hy * 8 + comp, ny, stride=8), :]
                out_v[comp, z, :, lanes] = tiles[h + z, hf, pl.ds(hy * 8 + 4 + comp, ny, stride=8), :]
        return c

    lax.fori_loop(0, nz, give, 0)


def solution(mesh):
    depths, lats = mesh.shape["depth"], mesh.shape["lat"]

    def per_device(disp, vel, inv, mat, dil_tab, shr_tab, stiff, imp, mask, inc):
        _, nz, ny, nx = disp.shape
        steps = inc.shape[0]
        w = min(WIDTH, nz, ny, steps)
        nh = nx // 128
        groups = -(-steps // w)
        ext_z = nz + 2 * w
        ext_y = -(-(-(-w // 8) * 8 + ny + w) // 8) * 8
        ndirs = (3 if depths > 1 else 1) * (3 if lats > 1 else 1) - 1
        smem = pl.BlockSpec(memory_space=pltpu.SMEM)
        vmem = pl.BlockSpec(memory_space=pltpu.VMEM)
        shape = jax.ShapeDtypeStruct(disp.shape, f32)
        return pl.pallas_call(
            functools.partial(kernel, (nz, ny, nx, steps, depths, lats, w)),
            out_shape=(shape, shape),
            in_specs=[smem] * 3 + [vmem] * 7,
            out_specs=(vmem, vmem),
            scratch_shapes=[
                pltpu.VMEM((ext_z, nh, ext_y, 8, 128), f32),
                pltpu.VMEM((ext_z, ext_y, 16, nx), bf16),
                pltpu.VMEM((2, ext_z, nh, ext_y, 128), f32),
                pltpu.VMEM((ext_y, 8, nx), f32),
                pltpu.VMEM((ext_y, 8, nx), f32),
                pltpu.VMEM((steps, nh, ext_y * 8, 128), f32),
                pltpu.VMEM((groups, 2, nz, nh, w, 8, 128), f32),
                pltpu.VMEM((groups, 2, w, nh, ny, 8, 128), f32),
                pltpu.VMEM((groups, 4, w, nh, w, 8, 128), f32),
                pltpu.VMEM((64, 128), bf16),
                pltpu.SemaphoreType.DMA((groups, ndirs, 2)),
                pltpu.SemaphoreType.DMA((groups, ndirs, 2)),
                pltpu.SemaphoreType.DMA((2,)),
                pltpu.SemaphoreType.DMA((2,)),
            ],
            compiler_params=pltpu.CompilerParams(
                collective_id=0, has_side_effects=True, vmem_limit_bytes=56 * 1024 * 1024
            ),
        )(dil_tab, shr_tab, imp, disp, vel, inv, mat, stiff, mask, inc)

    field = P(None, "depth", "lat", None)
    node = P("depth", "lat", None)
    in_specs = (field, field, node, node, P(), P(), P(), P(), P("lat", None), P(None, None, "lat", None))
    return jax.shard_map(
        per_device, mesh=mesh, in_specs=in_specs, out_specs=(field, field), check_vma=False
    )
```

time: 50.8 us -> 39.4 us (0.78)
  Pallas kernels: 47.6 us -> 36.3 us
    pallas_call x1, Pallas kernels: 47.6 us -> 36.3 us  [per_device(): pl.pallas_call(functools.partial(kernel, (nz, ny, nx, steps, depths, lats...]
where the time goes in v1:
time: 39.4 us; the launch traced here: 39.3 us
  Pallas kernels  36.3 us (92%)
  local copies, waits for them, and re-layouts  2.34 us (6%)
  between operations  0.65 us (2%)
    pallas_call x1, Pallas kernels, per_device(): pl.pallas_call(functools.partial(kernel, (nz, ny, nx, steps, depths, lats...  36.3 us
    unnamed x4, local copies, waits for them, and re-layouts  2.34 us

profile of v1, /device:TPU:19, one launch (start us, length us, event | category | flops | bytes accessed | tf_op | source)
XLA Modules:
  0.0 39.3 jit_solution(2886074375740076707)
XLA Ops:
  0.6 36.3 %shard_map.113 = (f32[3,8,8,256]{3,2,1,0:T(8,128)}, f32[3,8,8,256]{3,2,1,0:T(8,128)}) custom-call(f32[8]{0:T(128)} %dil_tab.1, f32[8]{0:T(128)} %shr_tab.1, f32[3]{0:T(128)} %imp_ref.1, f32[3,8,8,256]{3,2,1,0:T(8,128)} %disp.1, f32[3,8,8,256]{3,2,1,0:T(8,128)} %vel.1, f32[8,8,256]{2,1,0:T(8,128)} %inv.1, s32[8,8,256]{2,1,0:T(8,128)} %mat.1, ...), custom_call_target="tpu_custom_call" | custom-call | tf_op jit(solution)/shard_map/pallas_call | solution.py:387
  36.9 0.0 copy-start
  36.9 1.7 %copy.14 = f32[3,8,8,256]{3,2,1,0:T(8,128)} copy(f32[3,8,8,256]{3,2,1,0:T(8,128)} %get-tuple-element.4) | data formatting | bytes 393216
  38.6 0.0 copy-done
  38.6 0.7 %copy.15 = f32[3,8,8,256]{3,2,1,0:T(8,128)} copy(f32[3,8,8,256]{3,2,1,0:T(8,128)S(1)} %copy-done) | data formatting | bytes 393216
Async XLA Ops:
  36.9 1.7 %copy-start = (f32[3,8,8,256]{3,2,1,0:T(8,128)S(1)}, f32[3,8,8,256]{3,2,1,0:T(8,128)}, u32[]{:S(2)}) copy-start(f32[3,8,8,256]{3,2,1,0:T(8,128)} %get-tuple-element.5) | copy-start | bytes 589828

commit v2 on v1

--- a/solution.py
+++ b/solution.py
@@ -14,7 +14,7 @@
 
 
 def kernel(
-    cfg, dil_tab, shr_tab, imp_ref, disp, vel, inv, mat, stiff, mask, inc, out_d, out_v,
+    cfg, dil_tab, shr_tab, imp_ref, disp, vel, inv, mat, stiff, mask, inc, out,
     grid5, split, moduli, carry, held, pull, land_y, land_z, land_c, big_s,
     send_sem, recv_sem, q_send, q_recv,
 ):
@@ -68,7 +68,7 @@
             tiles[h + z, hf, pl.ds(hy * 8 + 7, ny, stride=8), :] = inv[z, :, lanes] * (-time_step)
         return c
 
-    lax.fori_loop(0, nz, fill_layer, 0)
+    lax.fori_loop(0, nz, fill_layer, 0, unroll=2)
 
     @pl.when(is_bottom)
     def _():
@@ -211,7 +211,7 @@
                     put_split(z0 + z, y0 + y, new)
                 return c
 
-            lax.fori_loop(0, zn, body, 0)
+            lax.fori_loop(0, zn, body, 0, unroll=zn)
 
     def sent(n):
         for dz, dy in dirs:
@@ -303,7 +303,7 @@
             put_split(h + z, hy + y, load_tile(h + z, hy + y))
         return c
 
-    lax.fori_loop(0, nz, split_layer, 0)
+    lax.fori_loop(0, nz, split_layer, 0, unroll=2)
 
     own_chunks = [y0 for y0 in range(0, ext_y, 8) if hy <= y0 and y0 + 8 <= hy + ny]
     other_chunks = [y0 for y0 in range(0, ext_y, 8) if y0 not in own_chunks]
@@ -325,14 +325,14 @@
 
         return body
 
-    lax.fori_loop(h, h + nz, lookup(own_chunks), 0)
+    lax.fori_loop(h, h + nz, lookup(own_chunks), 0, unroll=4)
 
     for s in range(steps):
         n, e = s // w, extra[s]
         if s % w == 0:
             if s > 0:
                 start_all(n)
-            for dz, dy in dirs:
+            for dz, dy in sorted(dirs, key=lambda d: (abs(d[0]) + abs(d[1]), abs(d[0]))):
                 receive(n, dz, dy)
             sent(n)
             if s == 0:
@@ -343,7 +343,7 @@
                         pull_copy(dy, True).wait_recv()
                 lax.fori_loop(0, h, lookup(own_chunks + other_chunks), 0)
                 lax.fori_loop(h + nz, ext_z, lookup(own_chunks + other_chunks), 0)
-                lax.fori_loop(h, h + nz, lookup(other_chunks), 0)
+                lax.fori_loop(h, h + nz, lookup(other_chunks), 0, unroll=2)
         start = jnp.where(di == 0, h, h - e)
         stop = jnp.where(is_bottom, h + nz - 1, h + nz - 1 + e)
         keep(products(start - 1, e, True))
@@ -362,11 +362,11 @@
         for hf in range(nh):
             lanes = slice(hf * 128, hf * 128 + 128)
             for comp in range(3):
-                out_d[comp, z, :, lanes] = tiles[h + z, hf, pl.ds(hy * 8 + comp, ny, stride=8), :]
-                out_v[comp, z, :, lanes] = tiles[h + z, hf, pl.ds(hy * 8 + 4 + comp, ny, stride=8), :]
+                out[0, comp, z, :, lanes] = tiles[h + z, hf, pl.ds(hy * 8 + comp, ny, stride=8), :]
+                out[1, comp, z, :, lanes] = tiles[h + z, hf, pl.ds(hy * 8 + 4 + comp, ny, stride=8), :]
         return c
 
-    lax.fori_loop(0, nz, give, 0)
+    lax.fori_loop(0, nz, give, 0, unroll=2)
 
 
 def solution(mesh):
@@ -384,11 +384,11 @@
         smem = pl.BlockSpec(memory_space=pltpu.SMEM)
         vmem = pl.BlockSpec(memory_space=pltpu.VMEM)
         shape = jax.ShapeDtypeStruct(disp.shape, f32)
-        return pl.pallas_call(
+        both = pl.pallas_call(
             functools.partial(kernel, (nz, ny, nx, steps, depths, lats, w)),
-            out_shape=(shape, shape),
+            out_shape=jax.ShapeDtypeStruct((2, *disp.shape), f32),
             in_specs=[smem] * 3 + [vmem] * 7,
-            out_specs=(vmem, vmem),
+            out_specs=vmem,
             scratch_shapes=[
                 pltpu.VMEM((ext_z, nh, ext_y, 8, 128), f32),
                 pltpu.VMEM((ext_z, ext_y, 16, nx), bf16),
@@ -409,6 +409,7 @@
                 collective_id=0, has_side_effects=True, vmem_limit_bytes=56 * 1024 * 1024
             ),
         )(dil_tab, shr_tab, imp, disp, vel, inv, mat, stiff, mask, inc)
+        return both[0], both[1]
 
     field = P(None, "depth", "lat", None)
     node = P("depth", "lat", None)

time: 39.4 us -> 36.1 us (0.916); the launches traced: 39.3 us -> 35.4 us
  Pallas kernels: 36.3 us -> 33 us
  local copies, waits for them, and re-layouts: 2.34 us -> 1.8 us
    pallas_call x1, Pallas kernels: 36.3 us -> 33 us  [per_device(): pl.pallas_call(functools.partial(kernel, (nz, ny, nx, steps, depths, lats...]
    unnamed x4 -> x0, local copies, waits for them, and re-layouts: 2.34 us -> none
    squeeze x0 -> x1, local copies, waits for them, and re-layouts: none -> 1.8 us  [per_device(): return (both[0], both[1])]
where the time goes in v2:
time: 36.1 us; the launch traced here: 35.4 us
  Pallas kernels  33 us (91%)
  local copies, waits for them, and re-layouts  1.8 us (5%)
  between operations  0.64 us (2%)
    pallas_call x1, Pallas kernels, per_device(): pl.pallas_call(functools.partial(kernel, (nz, ny, nx, steps, depths, lats...  33 us
    squeeze x1, local copies, waits for them, and re-layouts, per_device(): return (both[0], both[1])  1.8 us

profile of v2, /device:TPU:19, one launch (start us, length us, event | category | flops | bytes accessed | tf_op | source)
XLA Modules:
  0.0 35.4 jit_solution(13566082250407736837)
XLA Ops:
  0.6 33.0 %shard_map.113 = f32[2,3,8,8,256]{4,3,2,1,0:T(8,128)} custom-call(f32[8]{0:T(128)} %dil_tab.1, f32[8]{0:T(128)} %shr_tab.1, f32[3]{0:T(128)} %imp_ref.1, f32[3,8,8,256]{3,2,1,0:T(8,128)} %disp.1, f32[3,8,8,256]{3,2,1,0:T(8,128)} %vel.1, f32[8,8,256]{2,1,0:T(8,128)} %inv.1, s32[8,8,256]{2,1,0:T(8,128)} %mat.1, f32[2,24,24]{2,1,0:T(8,128)} %stiff.1, ...), custom_call_target="tpu_custom_call" | custom-call | tf_op jit(solution)/shard_map/pallas_call | solution.py:387
  33.6 1.8 %slice_bitcast_fusion = (f32[3,8,8,256]{3,2,1,0:T(8,128)}, f32[3,8,8,256]{3,2,1,0:T(8,128)}) fusion(f32[2,3,8,8,256]{4,3,2,1,0:T(8,128)} %shard_map.113), kind=kLoop, calls=%fused_computation | loop fusion | bytes 786432 | tf_op jit(solution)/shard_map/squeeze | solution.py:412
